TPU v7x, 8 devices: a whole 2x2x1 slice. The times are simulated.
8 devices in a mesh: dp: 1 (over z), depth: 2 (over y), col: 2 (over x), row: 2 (over core).
Axes of the slice: x: 2, y: 2, z: 1, core: 2. Of those that a mesh axis runs over, the one named last changes fastest.
Arguments:
- x_in: bfloat16 [32768, 1024], P(('dp', 'depth', 'row'), 'col')
- ln_gamma: float32 [1024], P('col')
- ln_beta: float32 [1024], P('col')
- w_up: bfloat16 [1024, 4096], P('row', 'col')
- b_up: bfloat16 [4096], P('col')
- w_down: bfloat16 [4096, 1024], P('row', 'col')
- b_down: bfloat16 [1024], P('col')
- grad_out: bfloat16 [32768, 1024], P(('dp', 'depth', 'row'), 'col')
Outputs:
- output 1: bfloat16 [32768, 1024], P(('dp', 'depth', 'row'), 'col')
- output 2: bfloat16 [32768, 1024], P(('dp', 'depth', 'row'), 'col')
- output 3: float32 [1024], P(('dp', 'col'))
- output 4: float32 [1024], P(('dp', 'col'))
- output 5: bfloat16 [1024, 4096], P(('dp', 'row'), 'col')
- output 6: float32 [4096], P(('dp', 'col'))
- output 7: bfloat16 [4096, 1024], P(('dp', 'row'), 'col')
- output 8: float32 [1024], P(('dp', 'col'))
All inputs are finite; a program needn't handle non-finite values.
Results may differ from a plain program's by a relative error of at most 0.0111409.
Values are sent between devices in bfloat16 or wider.
A program may use at most 1 GiB of HBM per device.

v0:
```python
import jax
import jax.numpy as jnp
from jax import lax
from jax.sharding import PartitionSpec as P

LN_EPS = 1e-5


def gelu_tanh(values):
    return jax.nn.gelu(values, approximate=True)


def solution(mesh):
    col_size = mesh.shape['col']
    token_axes = ('depth', 'row')
    tok_spec = P(('dp', 'depth', 'row'), 'col')
    vec_spec = P('col')
    mat_spec = P('row', 'col')
    grad_vec = P(('dp', 'col'))
    grad_mat = P(('dp', 'row'), 'col')

    def local_pass(x_blk, gamma_blk, beta_blk, w_up_blk, b_up_blk, w_down_blk, b_down_blk, dy_blk):
        inv_width = 1.0 / (x_blk.shape[1] * col_size)
        x_f32 = x_blk.astype(jnp.float32)
        row_mean = lax.psum(jnp.sum(x_f32, axis=1, keepdims=True), 'col') * inv_width
        centered = x_f32 - row_mean
        row_var = lax.psum(jnp.sum(centered * centered, axis=1, keepdims=True), 'col') * inv_width
        inv_std = lax.rsqrt(row_var + LN_EPS)
        x_hat = centered * inv_std
        x_norm = (x_hat * gamma_blk + beta_blk).astype(jnp.bfloat16)
        norm_rows = lax.all_gather(x_norm, 'col', axis=1, tiled=True)
        w_up_cols = lax.all_gather(w_up_blk, 'row', axis=0, tiled=True)
        pre_act = (jnp.dot(norm_rows, w_up_cols, preferred_element_type=jnp.float32) + b_up_blk.astype(jnp.float32)).astype(jnp.bfloat16)
        act_f32, gelu_vjp = jax.vjp(gelu_tanh, pre_act.astype(jnp.float32))
        hidden = act_f32.astype(jnp.bfloat16)
        hidden_rows = lax.all_gather(hidden, 'col', axis=1, tiled=True)
        w_down_cols = lax.all_gather(w_down_blk, 'row', axis=0, tiled=True)
        y_blk = (x_f32 + jnp.dot(hidden_rows, w_down_cols, preferred_element_type=jnp.float32) + b_down_blk.astype(jnp.float32)).astype(jnp.bfloat16)
        dy_f32 = dy_blk.astype(jnp.float32)
        grad_b_down = lax.psum(jnp.sum(dy_f32, axis=0), token_axes)
        down_part = jnp.einsum('tf,th->fh', hidden_rows, dy_blk, preferred_element_type=jnp.float32)
        grad_w_down = lax.psum(lax.psum_scatter(down_part, 'row', scatter_dimension=0, tiled=True), 'depth').astype(jnp.bfloat16)
        hidden_part = jnp.einsum('th,fh->tf', dy_blk, w_down_cols, preferred_element_type=jnp.float32)
        grad_hidden = lax.psum_scatter(hidden_part, 'col', scatter_dimension=1, tiled=True)
        grad_pre = gelu_vjp(grad_hidden)[0].astype(jnp.bfloat16)
        grad_b_up = lax.psum(jnp.sum(grad_pre.astype(jnp.float32), axis=0), token_axes)
        up_part = jnp.einsum('th,tf->hf', norm_rows, grad_pre, preferred_element_type=jnp.float32)
        grad_w_up = lax.psum(lax.psum_scatter(up_part, 'row', scatter_dimension=0, tiled=True), 'depth').astype(jnp.bfloat16)
        norm_part = jnp.einsum('tf,hf->th', grad_pre, w_up_cols, preferred_element_type=jnp.float32)
        grad_norm = lax.psum_scatter(norm_part, 'col', scatter_dimension=1, tiled=True)
        grad_gamma = lax.psum(jnp.sum(grad_norm * x_hat, axis=0), token_axes)
        grad_beta = lax.psum(jnp.sum(grad_norm, axis=0), token_axes)
        grad_hat = grad_norm * gamma_blk
        sum_plain, sum_proj = lax.psum((jnp.sum(grad_hat, axis=1, keepdims=True), jnp.sum(grad_hat * x_hat, axis=1, keepdims=True)), 'col')
        grad_x = (dy_f32 + inv_std * (grad_hat - sum_plain * inv_width - x_hat * (sum_proj * inv_width))).astype(jnp.bfloat16)
        return y_blk, grad_x, grad_gamma, grad_beta, grad_w_up, grad_b_up, grad_w_down, grad_b_down

    return jax.shard_map(
        local_pass,
        mesh=mesh,
        in_specs=(tok_spec, vec_spec, vec_spec, mat_spec, vec_spec, mat_spec, vec_spec, tok_spec),
        out_specs=(tok_spec, tok_spec, grad_vec, grad_vec, grad_mat, grad_vec, grad_mat, grad_vec),
        check_vma=False,
    )
```

profile of v0, /device:TPU:0, one launch (start us, length us, event | category | flops | bytes accessed | tf_op | source)
XLA Modules:
  0.0 3274.9 jit_solution(14615913851933626360)
XLA Ops:
  7.2 0.0 copy-start.8
  7.2 0.0 copy-start.4
  7.2 0.0 all-gather.11.cloned.1.call-start
  7.2 0.7 all-gather.11.cloned.1.call-update
  7.9 0.0 all-gather.7.cloned.1.call-start
  8.0 0.7 all-gather.7.cloned.1.call-update
  8.7 0.0 all-gather.5.cloned.1.call-start
  8.7 4.6 convert_reduce_fusion.1
  13.3 10.3 psum.70
  23.7 0.0 copy-start
  23.7 6.0 fusion.22
  29.7 6.9 psum.71
  36.6 0.1 add_rsqrt_fusion
  36.7 0.0 copy-start.2
  36.7 0.6 copy-done.2
  37.3 0.0 copy-done.8
  37.3 0.0 copy-done.4
  37.3 8.5 fusion.17
  45.8 0.0 all-gather.5.cloned.1.call-update
  45.8 0.0 copy-done
  45.8 0.0 reduce-scatter.5.cloned.1.call-start
  45.9 0.0 all-gather.11.cloned.1.call-done
  45.9 51.7 %fusion.27 = f32[8192,4096]{1,0:T(8,128)} fusion(bf16[8192,512]{1,0:T(8,128)(2,1)} %param.15, bf16[4096,512]{1,0:T(8,128)(2,1)} %all-gather.11.cloned.1.call-done), kind=kOutput, calls=%fused_computation.43 | convolution fusion | flops 34359738368 | bytes 146800640 | tf_op jit(solution)/shard_map/th,fh->tf/dot_general | solution.py:43
  97.6 0.0 copy-start.7
  97.6 0.0 reduce-scatter.5.cloned.1.call-update
  97.7 0.6 reduce-scatter.7.cloned.1.call-start
  98.2 0.1 copy-done.7
  98.3 0.0 all-gather.7.cloned.1.call-done
  98.3 145.7 %all-gather.5.cloned.1.call-done = bf16[8192,1024]{1,0:T(8,128)(2,1)} async-done(((bf16[8192,512]{1,0:T(8,128)(2,1)}), bf16[8192,1024]{1,0:T(8,128)(2,1)}) %all-gather.5.cloned.1.call-update) | async-done | bytes 16777232 | tf_op jit(solution)/shard_map/all_gather | solution.py:31
  244.0 1446.8 %reduce-scatter.5.cloned.1.call-done = f32[8192,2048]{1,0:T(8,128)} async-done(((f32[8192,4096]{1,0:T(8,128)}), f32[8192,2048]{1,0:T(8,128)}) %reduce-scatter.5.cloned.1.call-update) | async-done | bytes 67108880 | tf_op jit(solution)/shard_map/reduce_scatter | solution.py:44
  1690.8 91.1 %convert_reduce_fusion = (f32[2048]{0:T(1024)}, bf16[8192,2048]{1,0:T(8,128)(2,1)}, bf16[8192,2048]{1,0:T(8,128)(2,1)}) fusion(f32[8192,2048]{1,0:T(8,128)} %reduce-scatter.5.cloned.1.call-done, f32[2048]{0:T(1024)S(1)} %convert_element_type.44, bf16[8192,1024]{1,0:T(8,128)(2,1)} %all-gather.5.cloned.1.call-done, ...), kind=kOutput, calls=%fused_computation.15 | convolution fusion | flops 34812723200 | bytes 155205632 | tf_op jit(solution)/shard_map/dot_general | solution.py:33
  1781.9 42.7 %fusion.28 = f32[8192,1024]{1,0:T(8,128)} fusion(bf16[8192,2048]{1,0:T(8,128)(2,1)} %get-tuple-element.21, bf16[1024,2048]{1,0:T(8,128)(2,1)} %all-gather.7.cloned.1.call-done), kind=kOutput, calls=%fused_computation.44 | convolution fusion | flops 34359738368 | bytes 71303168 | tf_op jit(solution)/shard_map/tf,hf->th/dot_general | solution.py:49
  1824.6 0.0 reduce-scatter.7.cloned.1.call-update
  1824.6 0.0 all-gather.9.cloned.1.call-start
  1824.7 0.5 all-gather.9.cloned.1.call-update
  1825.2 0.0 copy-start.1
  1825.2 0.0 copy-start.3
  1825.2 0.0 copy-start.5
  1825.2 0.0 reduce-scatter.9.cloned.1.call-start
  1825.3 43.9 %fusion.29 = f32[1024,2048]{1,0:T(8,128)} fusion(bf16[8192,1024]{1,0:T(8,128)(2,1)} %all-gather.5.cloned.1.call-done, bf16[8192,2048]{1,0:T(8,128)(2,1)} %get-tuple-element.21), kind=kOutput, calls=%fused_computation.45 | convolution fusion | flops 34359738368 | bytes 58720256 | tf_op jit(solution)/shard_map/th,tf->hf/dot_general | solution.py:47
  1869.2 0.0 reduce-scatter.9.cloned.1.call-update
  1869.2 0.0 all-reduce.6.cloned.1.call-start
  1869.3 321.6 %reduce-scatter.7.cloned.1.call-done = f32[8192,512]{1,0:T(8,128)} async-done(((f32[8192,1024]{1,0:T(8,128)}), f32[8192,512]{1,0:T(8,128)}) %reduce-scatter.7.cloned.1.call-update) | async-done | bytes 16777232 | tf_op jit(solution)/shard_map/reduce_scatter | solution.py:50
  2190.8 0.0 copy-done.1
  2190.8 0.0 copy-done.3
  2190.8 0.0 copy-done.5
  2190.8 12.7 fusion.21
  2203.5 0.0 all-reduce.6.cloned.1.call-update
  2203.6 0.0 copy-start.9
  2203.6 0.0 reduce-scatter.11.cloned.1.call-start
  2203.6 751.8 %all-gather.9.cloned.1.call-done = bf16[8192,4096]{1,0:T(8,128)(2,1)} async-done(((bf16[8192,2048]{1,0:T(8,128)(2,1)}), bf16[8192,4096]{1,0:T(8,128)(2,1)}) %all-gather.9.cloned.1.call-update) | async-done | bytes 67108880 | tf_op jit(solution)/shard_map/all_gather | solution.py:36
  2955.4 45.0 %fusion.30 = f32[4096,512]{1,0:T(8,128)} fusion(bf16[8192,4096]{1,0:T(8,128)(2,1)} %all-gather.9.cloned.1.call-done, bf16[8192,512]{1,0:T(8,128)(2,1)} %param.15), kind=kOutput, calls=%fused_computation.46 | convolution fusion | flops 34359738368 | bytes 83886080 | tf_op jit(solution)/shard_map/tf,th->fh/dot_general | solution.py:41
  3000.4 0.0 reduce-scatter.11.cloned.1.call-update
  3000.5 0.0 copy-done.9
  3000.5 0.0 reduce-scatter.9.cloned.1.call-done
  3000.5 45.2 %fusion.25 = bf16[8192,512]{1,0:T(8,128)(2,1)} fusion(bf16[8192,512]{1,0:T(8,128)(2,1)} %param.8, bf16[8192,4096]{1,0:T(8,128)(2,1)} %all-gather.9.cloned.1.call-done, bf16[4096,512]{1,0:T(8,128)(2,1)} %all-gather.11.cloned.1.call-done, f32[512]{0:T(512)S(1)} %convert_element_type.48), kind=kOutput, calls=%fused_computation.37 | convolution fusion | flops 34376515584 | bytes 88082432 | tf_op jit(solution)/shard_map/dot_general | solution.py:38
  3045.7 0.0 all-reduce.6.cloned.1.call-done
  3045.7 0.8 broadcast_multiply_fusion
  3046.6 0.0 copy-start.6
  3046.6 17.5 convert_reduce_fusion.2
  3064.0 0.0 copy-done.6
  3064.0 11.2 all-reduce
  3075.3 0.0 reduce-scatter.11.cloned.1.call-done
  3075.3 192.6 %all-reduce.7 = (bf16[512,2048]{1,0:T(8,128)(2,1)}, bf16[2048,512]{1,0:T(8,128)(2,1)}) all-reduce(f32[512,2048]{1,0:T(8,128)} %reduce-scatter.9.cloned.1.call-done, f32[2048,512]{1,0:T(8,128)} %reduce-scatter.11.cloned.1.call-done), channel_id=1, replica_groups=mesh['dp'=1,'depth'=2,'col'=2,'row'=2] {'depth'}, use_global_device_ids=true, to_apply=%region_15.0 | all-reduce | flops 2097152 | bytes 12582912 | tf_op jit(solution)/shard_map/psum | solution.py:48
  (3 shorter events, 0.0 us)
Async XLA Ops:
  7.2 30.1 copy-start.8
  7.2 30.1 copy-start.4
  7.2 38.7 %all-gather.11.cloned.1.call-start = ((), (), s32[]{:S(2)}) async-start(), calls=%async_computation.7 | async-start | bytes 6291456 | tf_op jit(solution)/shard_map/all_gather | solution.py:37
  7.9 90.4 %all-gather.7.cloned.1.call-start = ((), (), s32[]{:S(2)}) async-start(), calls=%async_computation.5 | async-start | bytes 6291456 | tf_op jit(solution)/shard_map/all_gather | solution.py:32
  8.7 235.3 %all-gather.5.cloned.1.call-start = ((), (), s32[]{:S(2)}) async-start(), calls=%async_computation.4 | async-start | bytes 25165824 | tf_op jit(solution)/shard_map/all_gather | solution.py:31
  23.7 22.2 copy-start
  36.7 0.6 copy-start.2
  45.8 1645.0 %reduce-scatter.5.cloned.1.call-start = ((), (), s32[]{:S(2)}) async-start(), calls=%async_computation.8 | async-start | bytes 201326592 | tf_op jit(solution)/shard_map/reduce_scatter | solution.py:44
  97.6 0.7 copy-start.7
  97.7 2093.2 %reduce-scatter.7.cloned.1.call-start = ((), (), s32[]{:S(2)}) async-start(), calls=%async_computation.9 | async-start | bytes 50331648 | tf_op jit(solution)/shard_map/reduce_scatter | solution.py:50
  1824.6 1130.8 %all-gather.9.cloned.1.call-start = ((), (), s32[]{:S(2)}) async-start(), calls=%async_computation.6 | async-start | bytes 100663296 | tf_op jit(solution)/shard_map/all_gather | solution.py:36
  1825.2 365.7 %copy-start.1 = (f32[8192,1]{0,1:T(1,128)S(1)}, f32[8192,1]{0,1:T(1,128)}, u32[]{:S(2)}) copy-start(f32[8192,1]{0,1:T(1,128)} %copy-done) | copy-start | bytes 98308
  1825.2 365.6 %copy-start.3 = (f32[8192,1]{0,1:T(1,128)S(1)}, f32[8192,1]{0,1:T(1,128)}, u32[]{:S(2)}) copy-start(f32[8192,1]{0,1:T(1,128)} %copy-done.2) | copy-start | bytes 98308
  1825.2 365.6 %copy-start.5 = (f32[512]{0:T(512)S(1)}, f32[512]{0:T(512)}, u32[]{:S(2)}) copy-start(f32[512]{0:T(512)} %param.9) | copy-start | bytes 6148
  1825.2 1175.3 %reduce-scatter.9.cloned.1.call-start = ((), (), s32[]{:S(2)}) async-start(), calls=%async_computation.10 | async-start | bytes 12582912 | tf_op jit(solution)/shard_map/reduce_scatter | solution.py:48
  1869.2 1176.5 %all-reduce.6.cloned.1.call-start = ((), (), s32[]{:S(2)}) async-start(), calls=%async_computation.12 | async-start | bytes 131072 | tf_op jit(solution)/shard_map/psum | solution.py:54
  2203.6 796.9 %copy-start.9 = (bf16[512]{0:T(512)(128)(2,1)S(1)}, bf16[512]{0:T(512)(128)(2,1)}, u32[]{:S(2)}) copy-start(bf16[512]{0:T(512)(128)(2,1)} %param.14) | copy-start | bytes 3076
  2203.6 871.7 %reduce-scatter.11.cloned.1.call-start = ((), (), s32[]{:S(2)}) async-start(), calls=%async_computation.11 | async-start | bytes 12582912 | tf_op jit(solution)/shard_map/reduce_scatter | solution.py:42
  3046.6 17.5 copy-start.6
Sparse Core Ops, SparseCore 0:
  9.5 14.0 all-gather.10
  25.1 12.3 all-gather.6
  45.9 198.0 all-gather.4
  246.1 1444.6 reduce-scatter.4
  1824.7 366.0 reduce-scatter.6
  2192.2 763.1 all-gather.8
  2958.2 13.1 reduce-scatter.8
  2974.3 16.4 all-reduce.5
  3000.6 13.1 reduce-scatter.10
where the time goes:
time: 3280 us; the launch traced here: 3270 us
  waiting for transfers between devices  2670 us (81%)
  matrix products  320 us (10%)
  blocking collectives  221 us (7%)
  other arithmetic  50.2 us (2%)
    reduce_scatter x1, waiting for transfers between devices, local_pass(): lax.psum_scatter(hidden_part, 'col', scatter_dimension=1, tiled=True)  1450 us
    all_gather x1, waiting for transfers between devices, local_pass(): hidden_rows = lax.all_gather(hidden, 'col', axis=1, tiled=True)  752 us
    reduce_scatter x1, waiting for transfers between devices, local_pass(): lax.psum_scatter(norm_part, 'col', scatter_dimension=1, tiled=True)  322 us
    psum x1, blocking collectives, local_pass(): lax.psum(lax.psum_scatter(up_part, 'row', scatter_dimension=0, tiled=True...  193 us
    all_gather x1, waiting for transfers between devices, local_pass(): norm_rows = lax.all_gather(x_norm, 'col', axis=1, tiled=True)  146 us
    dot_general x1, matrix products, local_pass(): jnp.dot(norm_rows, w_up_cols, preferred_element_type=jnp.float32)  91.1 us
  transfers between devices with their start and end apart: 9, of which 4 were waited for; matrix products, arithmetic and copies ran while one was open for 7% of the time, Pallas kernels for 0%

commit v1 on v0

v1 whole, which is shorter than its diff:
```python
import functools

import jax
import jax.numpy as jnp
from jax import lax
from jax.experimental import pallas as pl
from jax.experimental.pallas import tpu as pltpu
from jax.sharding import PartitionSpec as P

LN_EPS = 1e-5
C0 = 0.7978845608
C1 = C0 * 0.044715
M = 512
FT = 512
SUBS = 4
BF16, F32 = jnp.bfloat16, jnp.float32
MESH = pl.DeviceIdType.MESH


def dot(lhs, rhs, lhs_dim, rhs_dim):
    return lax.dot_general(lhs, rhs, (((lhs_dim,), (rhs_dim,)), ((), ())), preferred_element_type=F32)


def gelu(v):
    t = jnp.tanh(v * (C1 * (v * v) + C0))
    h = 0.5 * v
    return h * t + h


def gelu_slope(v):
    v2 = v * v
    t = jnp.tanh(v * (C1 * v2 + C0))
    return (v * (1.0 - t * t)) * (1.5 * C1 * v2 + 0.5 * C0) + (0.5 * t + 0.5)


def fold8(v):
    return jnp.sum(v.reshape(v.shape[0] // 8, 8, v.shape[1]), axis=0)


def kernel(x_h, dy_h, wu_h, wd_h, sm_h,
           y_h, dx_h, gwu_h, gwd_h, gs_h, u_h, xn_h, st_h, dxn_h, rdown_h, ydown_h,
           wu, wd, acc_d, acc_u, own, land, aux, xn2, tr, ub, st, da_s, act, acc, yo,
           bup8, gb8, smv, s12, s12o, gd_s, gu_s, gsp, gsl,
           w_sem, wrow_s, wrow_r, wx_s, wx_r, wy_s, wy_r, wa_s, wa_r, wb_s, wb_r,
           sm_sem, land_s, land_r, ld_sem, out_sem, rd_sem, yd_sem, dl_sem, gd_sem,
           ru_s, ru_r, yu_s, yu_r, gu_s_sem, gu_r_sem, s12_sem, gs_sem, credit, free_row, free_dep):
    chunks = x_h.shape[0] // M
    half_f = wu_h.shape[1]
    hw = x_h.shape[1]
    full = 2 * hw
    tiles = 2 * half_f // FT
    c, r, d = lax.axis_index('col'), lax.axis_index('row'), lax.axis_index('depth')
    b = lax.rem(r + c, 2)
    peer = {'col': 1 - c, 'row': 1 - r, 'depth': 1 - d}

    def send(src, dst, s_sem, r_sem, axis):
        return pltpu.make_async_remote_copy(src_ref=src, dst_ref=dst, send_sem=s_sem, recv_sem=r_sem,
                                            device_id={axis: peer[axis]}, device_id_type=MESH)

    def local(src, dst, sem):
        return pltpu.make_async_copy(src, dst, sem)

    def rows_of(k):
        return pl.ds(pl.multiple_of(k * M, M), M)

    bar = pltpu.get_barrier_semaphore()
    for axis in ('col', 'row', 'depth'):
        pl.semaphore_signal(bar, inc=1, device_id={axis: peer[axis]}, device_id_type=MESH)
    pl.semaphore_wait(bar, 3)

    def w_cols(kind, blk, dep, s):
        if kind == 0:
            n = half_rows_u // SUBS
            return wu.at[pl.ds(pl.multiple_of(blk * hw + dep * half_rows_u + s * n, n), n), pl.ds(half_f, half_f)]
        n = half_rows_d // SUBS
        return wd.at[pl.ds(pl.multiple_of(blk * half_f + dep * half_rows_d + s * n, n), n), pl.ds(hw, hw)]

    half_rows_u, half_rows_d = hw // 2, half_f // 2
    w_srcs = (wu_h, wd_h)

    def w_src(kind, s):
        half = (half_rows_u, half_rows_d)[kind]
        n = half // SUBS
        return w_srcs[kind].at[pl.ds(pl.multiple_of(d * half + s * n, n), n), :]

    def w_own(kind):
        if kind == 0:
            return wu.at[pl.ds(pl.multiple_of(b * hw, hw), hw), pl.ds(0, half_f)]
        return wd.at[pl.ds(pl.multiple_of(b * half_f, half_f), half_f), pl.ds(0, hw)]

    def w_x(kind, s):
        return send(w_src(kind, s), w_cols(kind, 1 - b, d, s), wx_s.at[kind, s], wx_r.at[kind, s], 'col')

    def w_y(kind, s):
        return send(w_cols(kind, b, d, s), w_cols(kind, b, d, s), wy_s.at[kind, s], wy_r.at[kind, s], 'depth')

    def w_a(kind, s):
        return send(w_cols(kind, b, d, s), w_cols(kind, b, d, s), wa_s.at[kind, s], wa_r.at[kind, s], 'row')

    def w_b(kind, s):
        return send(w_cols(kind, b, 1 - d, s), w_cols(kind, b, 1 - d, s), wb_s.at[kind, s], wb_r.at[kind, s], 'row')

    def w_row(kind):
        return send(w_srcs[kind], w_own(kind), wrow_s.at[kind], wrow_r.at[kind], 'row')

    def w_load(kind):
        return local(w_srcs[kind], w_own(kind), w_sem.at[kind])

    def w_forward(kind):
        for s in range(SUBS):
            w_x(kind, s).wait_recv()
            w_y(kind, s).start()
            w_a(kind, s).start()
        for s in range(SUBS):
            w_y(kind, s).wait_recv()
            w_b(kind, s).start()
        for s in range(SUBS):
            w_a(kind, s).wait_recv()
            w_b(kind, s).wait_recv()
        for s in range(SUBS):
            w_x(kind, s).wait_send()
            w_y(kind, s).wait_send()
            w_a(kind, s).wait_send()
            w_b(kind, s).wait_send()

    def stream(src, k, q):
        slot = lax.rem(q, 4)
        return send(src.at[rows_of(k), :], land.at[slot], land_s.at[slot], land_r.at[slot], 'col')

    def stream_next(src, k, q):
        @pl.when(q >= 4)
        def _():
            stream(src, k, q).wait_send()
            pl.semaphore_wait(credit, 1)
        stream(src, k, q).start()

    for s in range(SUBS):
        w_x(0, s).start()
    sm_out = send(sm_h, smv.at[1], sm_sem.at[0], sm_sem.at[1], 'col')
    sm_own = local(sm_h, smv.at[0], sm_sem.at[2])
    sm_out.start()
    sm_own.start()
    for kind in range(2):
        w_load(kind).start()
        w_row(kind).start()
    stream(x_h, 0, 0).start()
    stream(x_h, 1, 1).start()

    def load_f(k):
        s = lax.rem(k, 2)
        return (local(x_h.at[rows_of(k), :], own.at[s], ld_sem.at[0, s]),
                local(dy_h.at[rows_of(k), :], aux.at[s], ld_sem.at[1, s]))

    for cp in load_f(0):
        cp.start()

    acc_d[...] = jnp.zeros_like(acc_d)
    acc_u[...] = jnp.zeros_like(acc_u)
    bup8[...] = jnp.zeros_like(bup8)
    gb8[...] = jnp.zeros_like(gb8)

    for kind in range(2):
        w_load(kind).wait()
        w_row(kind).wait()
    sm_own.wait()
    sm_out.wait()
    w_forward(0)

    def out_f(k):
        s = lax.rem(k, 2)
        return (local(ub.at[s], u_h.at[rows_of(k), :], out_sem.at[0, s]),
                local(xn2.at[s], xn_h.at[rows_of(k), :], out_sem.at[1, s]),
                local(st.at[s], st_h.at[rows_of(k), :], out_sem.at[2, s]),
                local(yo.at[s], y_h.at[rows_of(k), :], out_sem.at[3, s]))

    def chunk_f(k, carry):
        s = lax.rem(k, 2)
        slot = lax.rem(k, 4)

        @pl.when(k < chunks - 2)
        def _():
            stream_next(x_h, k + 2, k + 2)

        @pl.when(k == chunks - 2)
        def _():
            for p in range(SUBS):
                w_x(1, p).start()

        @pl.when(k == chunks - 1)
        def _():
            stream_next(dy_h, k - (chunks - 1), k + 1)

        for cp in load_f(k):
            cp.wait()

        @pl.when(k < chunks - 1)
        def _():
            for cp in load_f(k + 1):
                cp.start()

        @pl.when(k >= 2)
        def _():
            for cp in out_f(k):
                cp.wait()

        stream(x_h, k, k).wait_recv()

        gam = jnp.concatenate([smv[0, 1:2, :hw], smv[1, 1:2, :hw]], axis=1)
        bet = jnp.concatenate([smv[0, 1:2, hw:full], smv[1, 1:2, hw:full]], axis=1)
        step = 32
        for i in range(M // step):
            rs = slice(i * step, (i + 1) * step)
            xv = jnp.concatenate([own[s, rs, :], land[slot, rs, :]], axis=1).astype(F32)
            mean = jnp.sum(xv, axis=1, keepdims=True) * (1.0 / full)
            cen = xv - mean
            istd = lax.rsqrt(jnp.sum(cen * cen, axis=1, keepdims=True) * (1.0 / full) + LN_EPS)
            xn2[s, rs, :] = (cen * istd * gam + bet).astype(BF16)
            st[s, rs, :] = jnp.concatenate([jnp.broadcast_to(mean, (step, 64)), jnp.broadcast_to(istd, (step, 64))], axis=1)
        dyv = aux[s]
        tr[:hw, :] = dyv.T
        gb8[:, full:full + hw] += fold8(dyv.astype(F32))

        def up(j):
            js = slice(j * FT, (j + 1) * FT)
            side, at = divmod(j * FT, half_f)
            u = dot(xn2[s], wu[:, js], 1, 0) + smv[side, 0:1, at:at + FT]
            ub[s, :, js] = u.astype(BF16)

        def down(j):
            js = slice(j * FT, (j + 1) * FT)
            act[j % 2] = gelu(ub[s, :, js].astype(F32)).astype(BF16)
            part = dot(act[j % 2], wd[js, :hw], 1, 0)
            acc[...] = part if j == 0 else acc[...] + part
            blk, rest = divmod(j * FT, half_f)
            qt, at = divmod(rest, half_f // 2)
            acc_d[blk, qt, :, at:at + FT] += dot(tr[:hw, :], act[j % 2], 1, 0)

        up(0)
        for j in range(tiles):
            if j + 1 < tiles:
                up(j + 1)
            down(j)
        bdn = smv[0, 1:2, full:full + hw]
        yo[s] = (own[s].astype(F32) + acc[...] + bdn).astype(BF16)
        for cp in out_f(k):
            cp.start()
        pl.semaphore_signal(credit, inc=1, device_id={'col': peer['col']}, device_id_type=MESH)
        return carry

    lax.fori_loop(0, chunks, chunk_f, 0)

    rdown = send(acc_d.at[1 - b], rdown_h, rd_sem.at[0], rd_sem.at[1], 'row')
    rdown.start()
    stream_next(dy_h, 1, chunks + 1)
    for k in (chunks - 2, chunks - 1):
        for cp in out_f(k):
            cp.wait()

    def load_b(k):
        s = lax.rem(k, 2)
        rs = rows_of(k)
        return (local(dy_h.at[rs, :], own.at[s], ld_sem.at[0, s]),
                local(x_h.at[rs, :], aux.at[s], ld_sem.at[1, s]),
                local(u_h.at[rs, :], ub.at[s], ld_sem.at[2, s]),
                local(xn_h.at[rs, :], xn2.at[s], ld_sem.at[3, s]),
                local(st_h.at[rs, :], st.at[s], ld_sem.at[4, s]))

    for cp in load_b(0):
        cp.start()
    w_forward(1)

    rd_load = local(rdown_h, acc_d.at[1 - b], dl_sem.at[0])
    ydown = send(acc_d.at[b, 1 - d], ydown_h, yd_sem.at[0], yd_sem.at[1], 'depth')
    yd_load = local(ydown_h, acc_d.at[1 - b, 0], dl_sem.at[1])
    half_d = half_f // 2
    gd_rows = pl.ds(pl.multiple_of(d * half_d, half_d), half_d)
    gd_own = local(gd_s, gwd_h.at[gd_rows, :], gd_sem.at[0])
    gd_far = send(gd_s, gwd_h.at[gd_rows, :], gd_sem.at[1], gd_sem.at[2], 'depth')
    dxn_out = lambda k: local(acc, dxn_h.at[rows_of(k), :], out_sem.at[0, 0])

    def reduce_down(k):
        @pl.when(k == 1)
        def _():
            rdown.wait()
            rd_load.start()

        @pl.when(k == 2)
        def _():
            rd_load.wait()
            for q in range(2):
                for i in range(hw // 64):
                    rs = slice(i * 64, (i + 1) * 64)
                    acc_d[b, q, rs, :] += acc_d[1 - b, q, rs, :]

        @pl.when(k == 3)
        def _():
            ydown.start()

        @pl.when(k == 9)
        def _():
            ydown.wait()
            yd_load.start()

        @pl.when(k == 10)
        def _():
            yd_load.wait()
            for i in range(half_d // 128):
                cs = slice(i * 128, (i + 1) * 128)
                total = acc_d[b, d, :, cs] + acc_d[1 - b, 0, :, cs]
                gd_s[cs, :] = total.T.astype(BF16)

        @pl.when(k == 11)
        def _():
            gd_own.start()
            gd_far.start()
            pl.semaphore_signal(free_row, inc=1, device_id={'row': peer['row']}, device_id_type=MESH)
            pl.semaphore_signal(free_dep, inc=1, device_id={'depth': peer['depth']}, device_id_type=MESH)

    gam_own = lambda: smv[0, 1:2, :hw]

    def chunk_b(k, carry):
        s = lax.rem(k, 2)
        q = k + chunks
        slot = lax.rem(q, 4)

        @pl.when(k < chunks - 2)
        def _():
            stream_next(dy_h, k + 2, q + 2)

        reduce_down(k)
        for cp in load_b(k):
            cp.wait()

        @pl.when(k < chunks - 1)
        def _():
            for cp in load_b(k + 1):
                cp.start()

        @pl.when(k >= 1)
        def _():
            dxn_out(k).wait()

        stream(dy_h, k, q).wait_recv()
        tr[...] = xn2[s].T

        def grad(j):
            js = slice(j * FT, (j + 1) * FT)
            dyv = jnp.concatenate([own[s], land[slot]], axis=1)
            da_s[j % 2] = dot(dyv, wd[js, :], 1, 1)

        def back(j):
            js = slice(j * FT, (j + 1) * FT)
            du = (da_s[j % 2] * gelu_slope(ub[s, :, js].astype(F32))).astype(BF16)
            act[j % 2] = du
            if j * FT < half_f:
                bup8[:, js] += fold8(du.astype(F32))
            part = dot(act[j % 2], wu[:hw, js], 1, 1)
            acc[...] = part if j == 0 else acc[...] + part
            if j * FT < half_f:
                up = dot(tr[...], act[j % 2], 1, 0)
                for i in range(4):
                    acc_u[i // 2, i % 2, :, js] += up[i * (hw // 2):(i + 1) * (hw // 2)]

        grad(0)
        for j in range(tiles):
            if j + 1 < tiles:
                grad(j + 1)
            back(j)
        gam = gam_own()
        step = 128
        for i in range(M // step):
            rs = slice(i * step, (i + 1) * step)
            dxn = acc[rs, :]
            xh = (aux[s, rs, :].astype(F32) - st[s, rs, 0:1]) * st[s, rs, 64:65]
            px = dxn * xh
            gb8[:, :hw] += fold8(px)
            gb8[:, hw:full] += fold8(dxn)
            s1 = jnp.sum(dxn * gam, axis=1, keepdims=True)
            s2 = jnp.sum(px * gam, axis=1, keepdims=True)
            both = jnp.concatenate([jnp.broadcast_to(s1, (step, 64)), jnp.broadcast_to(s2, (step, 64))], axis=1).T
            s12[k, 0:4, rs] = both[0:4]
            s12[k, 4:8, rs] = both[64:68]
        dxn_out(k).start()

        @pl.when(k < chunks - 4)
        def _():
            pl.semaphore_signal(credit, inc=1, device_id={'col': peer['col']}, device_id_type=MESH)
        return carry

    lax.fori_loop(0, chunks, chunk_b, 0)

    pl.semaphore_wait(free_row, 1)
    pl.semaphore_wait(free_dep, 1)
    parts = half_f // FT
    hq = hw // 2

    def ru(p):
        dst = acc_d.at[0, :, pl.ds((p // 2) * hq, hq), pl.ds((p % 2) * FT, FT)]
        return send(acc_u.at[1 - b, :, :, pl.ds(p * FT, FT)], dst, ru_s.at[p], ru_r.at[p], 'row')

    def yu(p):
        dst = acc_d.at[1, p // 2, pl.ds(0, hq), pl.ds((p % 2) * FT, FT)]
        return send(acc_u.at[b, 1 - d, :, pl.ds(p * FT, FT)], dst, yu_s.at[p], yu_r.at[p], 'depth')

    gu_rows = pl.ds(pl.multiple_of(d * hq, hq), hq)

    def gu_far(p):
        ps = pl.ds(p * FT, FT)
        return send(gu_s.at[:, ps], gwu_h.at[gu_rows, ps], gu_s_sem.at[p], gu_r_sem.at[p], 'depth')

    gu_own = local(gu_s, gwu_h.at[gu_rows, :], gd_sem.at[3])
    for p in range(parts):
        ru(p).start()
    s12_x = send(s12, s12o, s12_sem.at[0], s12_sem.at[1], 'col')
    s12_x.start()
    gsp[0] = jnp.concatenate([jnp.sum(bup8[...], axis=0, keepdims=True), jnp.sum(gb8[...], axis=0, keepdims=True),
                              jnp.zeros((6, half_f), F32)], axis=0)
    gs_row = send(gsp.at[0], gsl.at[0], gs_sem.at[0], gs_sem.at[1], 'row')
    gs_row.start()
    dxn_out(chunks - 1).wait()

    def load_t(k):
        s = lax.rem(k, 2)
        rs = rows_of(k)
        return (local(dy_h.at[rs, :], own.at[s], ld_sem.at[0, s]),
                local(x_h.at[rs, :], aux.at[s], ld_sem.at[1, s]),
                local(dxn_h.at[rs, :], da_s.at[s], ld_sem.at[2, s]),
                local(st_h.at[rs, :], st.at[s], ld_sem.at[3, s]))

    for cp in load_t(0):
        cp.start()
    for p in range(parts):
        ru(p).wait_recv()
        for i in range(2):
            rs = slice((p // 2) * hq, (p // 2) * hq + hq)
            cs = slice((p % 2) * FT, (p % 2) * FT + FT)
            acc_u[b, i, :, p * FT:(p + 1) * FT] += acc_d[0, i, rs, cs]
        yu(p).start()
    gs_row.wait()
    gsp[1] = gsp[0] + gsl[0]
    gs_dep = send(gsp.at[1], gsl.at[1], gs_sem.at[2], gs_sem.at[3], 'depth')
    gs_dep.start()
    s12_x.wait()

    def out_t(k):
        s = lax.rem(k, 2)
        return local(yo.at[s], dx_h.at[rows_of(k), :], out_sem.at[3, s])

    def chunk_t(k, carry):
        s = lax.rem(k, 2)
        for cp in load_t(k):
            cp.wait()

        @pl.when(k < chunks - 1)
        def _():
            for cp in load_t(k + 1):
                cp.start()

        @pl.when(k >= 2)
        def _():
            out_t(k).wait()

        gam = gam_own()
        step = 128
        for i in range(M // step):
            rs = slice(i * step, (i + 1) * step)
            sums = (s12[k, :, rs] + s12o[k, :, rs]) * (1.0 / full)
            cols = jnp.concatenate([sums] * (step // 8), axis=0).T
            istd = st[s, rs, 64:65]
            xh = (aux[s, rs, :].astype(F32) - st[s, rs, 0:1]) * istd
            g = da_s[s, rs, :] * gam
            yo[s, rs, :] = (own[s, rs, :].astype(F32) + istd * (g - cols[:, 0:1] - xh * cols[:, 4:5])).astype(BF16)
        out_t(k).start()
        return carry

    lax.fori_loop(0, chunks, chunk_t, 0)
    gs_dep.wait()
    gsp[0] = gsp[1] + gsl[1]
    gs_out = local(gsp.at[0], gs_h, gs_sem.at[4])
    gs_out.start()
    for p in range(parts):
        yu(p).wait_recv()
        cs = slice((p % 2) * FT, (p % 2) * FT + FT)
        gu_s[:, p * FT:(p + 1) * FT] = (acc_u[b, d, :, p * FT:(p + 1) * FT] + acc_d[1, p // 2, 0:hq, cs]).astype(BF16)
        gu_far(p).start()
    gu_own.start()
    for k in (chunks - 2, chunks - 1):
        out_t(k).wait()
    gs_out.wait()
    gd_own.wait()
    gd_far.wait()
    for k in range(4):
        stream(dy_h, k, chunks + k).wait_send()
    for p in range(parts):
        ru(p).wait_send()
        yu(p).wait_send()
        gu_far(p).wait()
    gu_own.wait()


def solution(mesh):
    tok_spec = P(('dp', 'depth', 'row'), 'col')
    vec_spec = P('col')
    mat_spec = P('row', 'col')
    grad_vec = P(('dp', 'col'))
    grad_mat = P(('dp', 'row'), 'col')

    def local_pass(x, gamma, beta, w_up, b_up, w_down, b_down, dy):
        rows, hw = x.shape
        half_f = b_up.shape[0]
        full_f, full = 2 * half_f, 2 * hw
        chunks = rows // M
        small = jnp.zeros((8, half_f), F32)
        small = small.at[0, :].set(b_up.astype(F32))
        small = small.at[1, :].set(jnp.concatenate([gamma, beta, b_down.astype(F32), jnp.zeros((half_f - 3 * hw,), F32)]))
        hbm = pl.BlockSpec(memory_space=pltpu.HBM)
        sds = jax.ShapeDtypeStruct
        V, D = pltpu.VMEM, pltpu.SemaphoreType.DMA
        outs = [
            sds((rows, hw), BF16), sds((rows, hw), BF16), sds((hw, half_f), BF16), sds((half_f, hw), BF16), sds((8, half_f), F32),
            sds((rows, full_f), BF16), sds((rows, full), BF16), sds((rows, 128), F32), sds((rows, hw), F32),
            sds((2, hw, half_f // 2), F32), sds((hw, half_f // 2), F32),
        ]
        scratch = [
            V((full, full_f), BF16), V((full_f, full), BF16), V((2, 2, hw, half_f // 2), F32), V((2, 2, hw // 2, half_f), F32),
            V((2, M, hw), BF16), V((4, M, hw), BF16), V((2, M, hw), BF16), V((2, M, full), BF16), V((full, M), BF16),
            V((2, M, full_f), BF16), V((2, M, 128), F32), V((2, M, FT), F32), V((2, M, FT), BF16), V((M, hw), F32), V((2, M, hw), BF16),
            V((8, half_f), F32), V((8, half_f), F32), V((2, 8, half_f), F32), V((chunks, 8, M), F32), V((chunks, 8, M), F32),
            V((half_f // 2, hw), BF16), V((hw // 2, half_f), BF16), V((2, 8, half_f), F32), V((2, 8, half_f), F32),
            D((2,)), D((2,)), D((2,)), D((2, SUBS)), D((2, SUBS)), D((2, SUBS)), D((2, SUBS)), D((2, SUBS)), D((2, SUBS)), D((2, SUBS)), D((2, SUBS)),
            D((3,)), D((4,)), D((4,)), D((5, 2)), D((4, 2)), D((2,)), D((2,)), D((2,)), D((4,)),
            D((half_f // FT,)), D((half_f // FT,)), D((half_f // FT,)), D((half_f // FT,)), D((half_f // FT,)), D((half_f // FT,)), D((2,)), D((5,)),
            pltpu.SemaphoreType.REGULAR, pltpu.SemaphoreType.REGULAR, pltpu.SemaphoreType.REGULAR,
        ]
        res = pl.pallas_call(
            kernel,
            out_shape=outs,
            in_specs=[hbm] * 5,
            out_specs=[hbm] * len(outs),
            scratch_shapes=scratch,
            compiler_params=pltpu.CompilerParams(collective_id=0, has_side_effects=True, vmem_limit_bytes=67043328),
            cost_estimate=pl.CostEstimate(flops=16 * rows * full * full_f, bytes_accessed=2 ** 28, transcendentals=2 * rows * full_f),
            name='mlp_block',
        )(x, dy, w_up, w_down, small)
        y, dx, gwu, gwd, gs = res[:5]
        return (y, dx, gs[1, :hw], gs[1, hw:full], gwu, gs[0], gwd, gs[1, full:full + hw])

    return jax.shard_map(
        local_pass,
        mesh=mesh,
        in_specs=(tok_spec, vec_spec, vec_spec, mat_spec, vec_spec, mat_spec, vec_spec, tok_spec),
        out_specs=(tok_spec, tok_spec, grad_vec, grad_vec, grad_mat, grad_vec, grad_mat, grad_vec),
        check_vma=False,
    )
```

time: 3280 us -> 566 us (0.17)
  waiting for transfers between devices: 2670 us -> 0 us
  Pallas kernels: 0 us -> 540 us
  matrix products: 320 us -> 0 us
  blocking collectives: 221 us -> 0 us
  other arithmetic: 50.2 us -> 2.03 us
    reduce_scatter x4 -> x0, waiting for transfers between devices: 1770 us -> none  [the longest x1 1450 us: local_pass(): lax.psum_scatter(hidden_part, 'col', scatter_dimension=1, tiled=True)]
    all_gather x4 -> x0, waiting for transfers between devices: 897 us -> none  [the longest x1 752 us: local_pass(): hidden_rows = lax.all_gather(hidden, 'col', axis=1, tiled=True)]
    pallas_call x0 -> x1, Pallas kernels: none -> 540 us  [local_pass(): pl.pallas_call(kernel, out_shape=outs, in_specs=[hbm] * 5, out_specs=[hbm...]
    dot_general x6 -> x0, matrix products: 320 us -> none  [the longest x1 91.1 us: local_pass(): jnp.dot(norm_rows, w_up_cols, preferred_element_type=jnp.float32)]
    psum x4 -> x0, blocking collectives: 221 us -> none  [the longest x1 193 us: local_pass(): lax.psum(lax.psum_scatter(up_part, 'row', scatter_dimension=0, tiled=True...]
    reduce_sum x4 -> x0, other arithmetic: 40.7 us -> none  [the longest x1 17.5 us: local_pass(): grad_b_down = lax.psum(jnp.sum(dy_f32, axis=0), token_axes)]
  transfers between devices with their start and end apart: 9 -> 0, of which waited for: 4 -> 0; matrix products, arithmetic and copies ran while one was open for 7% -> 0% of each run, Pallas kernels for 0% -> 0%
where the time goes in v1:
time: 566 us; the launch traced here: 565 us
  Pallas kernels  540 us (95%)
  local copies, waits for them, and re-layouts  22.4 us (4%)
    pallas_call x1, Pallas kernels, local_pass(): pl.pallas_call(kernel, out_shape=outs, in_specs=[hbm] * 5, out_specs=[hbm...  540 us
    unnamed x8, local copies, waits for them, and re-layouts  17.5 us

profile of v1, /device:TPU:0, one launch (start us, length us, event | category | flops | bytes accessed | tf_op | source)
XLA Modules:
  0.0 565.1 jit_solution(17465570560511249158)
XLA Ops:
  0.6 0.7 convert_element_type.4
  1.3 0.7 pad_maximum_fusion
  2.0 0.7 reshape.69
  2.7 0.6 pad_convert_fusion
  3.4 1.5 scatter.14.sm_h
  4.8 540.0 %mlp_block.1 = (bf16[8192,512]{1,0:T(8,128)(2,1)}, bf16[8192,512]{1,0:T(8,128)(2,1)}, bf16[512,2048]{1,0:T(8,128)(2,1)}, bf16[2048,512]{1,0:T(8,128)(2,1)}, f32[...) custom-call(bf16[8192,512]{1,0:T(8,128)(2,1)} %x_h.1, ...), custom_call_target="tpu_custom_call" | custom-call | flops 549755813888 | bytes 268435456 | tf_op jit(solution)/shard_map/mlp_block/pallas_call | solution.py:535
  544.8 1.3 fusion
  546.2 1.4 slice.43
  547.6 7.3 %copy.21 = bf16[8192,512]{1,0:T(8,128)(2,1)} copy(bf16[8192,512]{1,0:T(8,128)(2,1)} %get-tuple-element.53) | data formatting | bytes 16777216
  554.9 0.0 copy-start.1
  554.9 0.0 copy-start
  554.9 7.5 %copy.22 = bf16[8192,512]{1,0:T(8,128)(2,1)} copy(bf16[8192,512]{1,0:T(8,128)(2,1)} %get-tuple-element.54) | data formatting | bytes 16777216
  562.4 0.0 copy-done.1
  562.4 1.3 copy.23
  563.7 0.0 copy-done
  563.7 1.3 copy.24
  (1 shorter events, 0.0 us)
Async XLA Ops:
  554.9 7.5 %copy-start.1 = (bf16[512,2048]{1,0:T(8,128)(2,1)S(1)}, bf16[512,2048]{1,0:T(8,128)(2,1)}, u32[]{:S(2)}) copy-start(bf16[512,2048]{1,0:T(8,128)(2,1)} %get-tuple-element.57) | copy-start | bytes 6291460
  554.9 8.8 %copy-start = (bf16[2048,512]{1,0:T(8,128)(2,1)S(1)}, bf16[2048,512]{1,0:T(8,128)(2,1)}, u32[]{:S(2)}) copy-start(bf16[2048,512]{1,0:T(8,128)(2,1)} %get-tuple-element.59) | copy-start | bytes 6291460
